TPU v7x, 32 devices: a whole 2x2x4 slice. The times are simulated.
32 devices in a mesh: rep: 8 (over z, core), tp: 4 (over y, x).
Axes of the slice: x: 2, y: 2, z: 4, core: 2. Of those that a mesh axis runs over, the one named last changes fastest.
Arguments:
- delta_query: bfloat16 [8, 2, 2048, 3072], P('rep', None, None, 'tp'), may hold values from -6 to 6
- master_query: float32 [2, 2048, 3072], P(None, 'rep', 'tp'), may hold values from -3 to 3
- moment_query: float32 [2, 2048, 3072], P(None, 'rep', 'tp'), may hold values from -3 to 3
- delta_latent: bfloat16 [8, 2, 512, 4096], P('rep', None, None, 'tp'), may hold values from -6 to 6
- master_latent: float32 [2, 512, 4096], P(None, 'rep', 'tp'), may hold values from -3 to 3
- moment_latent: float32 [2, 512, 4096], P(None, 'rep', 'tp'), may hold values from -3 to 3
- delta_output: bfloat16 [8, 2, 2048, 2048], P('rep', None, 'tp'), may hold values from -6 to 6
- master_output: float32 [2, 2048, 2048], P(None, 'tp', 'rep'), may hold values from -3 to 3
- moment_output: float32 [2, 2048, 2048], P(None, 'tp', 'rep'), may hold values from -3 to 3
Outputs:
- params_query: bfloat16 [2, 2048, 3072], P(None, None, 'tp')
- new_master_query: float32 [2, 2048, 3072], P(None, 'rep', 'tp')
- new_moment_query: float32 [2, 2048, 3072], P(None, 'rep', 'tp')
- params_latent: bfloat16 [2, 512, 4096], P(None, None, 'tp')
- new_master_latent: float32 [2, 512, 4096], P(None, 'rep', 'tp')
- new_moment_latent: float32 [2, 512, 4096], P(None, 'rep', 'tp')
- params_output: bfloat16 [2, 2048, 2048], P(None, 'tp')
- new_master_output: float32 [2, 2048, 2048], P(None, 'tp', 'rep')
- new_moment_output: float32 [2, 2048, 2048], P(None, 'tp', 'rep')
All inputs are finite; a program needn't handle non-finite values.
Results may differ from a plain program's by a relative error of at most 0.012.
Values may be sent and summed in bfloat16 or wider, within the bound.
No kernel may reach another device: no remote copies, remote signals or barrier semaphores. Data moves between devices by JAX's collectives and lax.ppermute only.
A program may use at most 128 MiB of HBM per device.

v0:
```python
import jax
import jax.numpy as jnp
from jax import lax
from jax.sharding import PartitionSpec as P

OUTER_RATE = 0.7
OUTER_MOMENTUM = 0.9


def nesterov(totals, master, moment, replica_count):
    average = totals / replica_count
    momentum = OUTER_MOMENTUM * moment + average
    updated = master - OUTER_RATE * (average + OUTER_MOMENTUM * momentum)
    return (updated, momentum)


def outer_step(
    delta_query,
    master_query,
    moment_query,
    delta_latent,
    master_latent,
    moment_latent,
    delta_output,
    master_output,
    moment_output,
):
    replica_count = lax.axis_size("rep")
    query_totals = lax.psum_scatter(
        delta_query[0].astype(jnp.float32).astype(jnp.bfloat16),
        "rep",
        scatter_dimension=1,
        tiled=True,
    ).astype(jnp.float32)
    latent_totals = lax.psum_scatter(
        delta_latent[0].astype(jnp.float32).astype(jnp.bfloat16),
        "rep",
        scatter_dimension=1,
        tiled=True,
    ).astype(jnp.float32)
    output_totals = lax.psum_scatter(
        delta_output[0].astype(jnp.float32).astype(jnp.bfloat16),
        "rep",
        scatter_dimension=2,
        tiled=True,
    ).astype(jnp.float32)
    query_master, query_moment = nesterov(query_totals, master_query, moment_query, replica_count)
    latent_master, latent_moment = nesterov(
        latent_totals, master_latent, moment_latent, replica_count
    )
    output_master, output_moment = nesterov(
        output_totals, master_output, moment_output, replica_count
    )
    query_params = lax.all_gather(query_master.astype(jnp.bfloat16), "rep", axis=1, tiled=True)
    latent_params = lax.all_gather(latent_master.astype(jnp.bfloat16), "rep", axis=1, tiled=True)
    output_params = lax.all_gather(output_master.astype(jnp.bfloat16), "rep", axis=2, tiled=True)
    return (
        query_params,
        query_master,
        query_moment,
        latent_params,
        latent_master,
        latent_moment,
        output_params,
        output_master,
        output_moment,
    )


def on_device(
    delta_query,
    master_query,
    moment_query,
    delta_latent,
    master_latent,
    moment_latent,
    delta_output,
    master_output,
    moment_output,
):
    return outer_step(
        delta_query,
        master_query,
        moment_query,
        delta_latent,
        master_latent,
        moment_latent,
        delta_output,
        master_output,
        moment_output,
    )


def solution(mesh):
    placed = (
        P("rep", None, None, "tp"),
        P(None, "rep", "tp"),
        P(None, "rep", "tp"),
        P("rep", None, None, "tp"),
        P(None, "rep", "tp"),
        P(None, "rep", "tp"),
        P("rep", None, "tp", None),
        P(None, "tp", "rep"),
        P(None, "tp", "rep"),
    )
    return jax.shard_map(
        on_device,
        mesh=mesh,
        in_specs=placed,
        out_specs=(
            P(None, None, "tp"),
            P(None, "rep", "tp"),
            P(None, "rep", "tp"),
            P(None, None, "tp"),
            P(None, "rep", "tp"),
            P(None, "rep", "tp"),
            P(None, "tp", None),
            P(None, "tp", "rep"),
            P(None, "tp", "rep"),
        ),
        check_vma=False,
    )
```

profile of v0, /device:TPU:0, one launch (start us, length us, event | category | flops | bytes accessed | tf_op | source)
XLA Modules:
  0.0 332.2 jit_solution(7297838098868273898)
XLA Ops:
  7.2 0.0 reduce-scatter.6.cloned.1.call-start
  7.2 0.7 reduce-scatter.6.cloned.1.call-update
  7.9 0.0 reduce-scatter.8.cloned.1.call-start
  8.0 0.7 reduce-scatter.8.cloned.1.call-update
  8.7 0.0 reduce-scatter.4.cloned.1.call-start
  8.7 0.0 copy-start.4
  8.7 0.0 copy-start.5
  8.7 0.7 reduce-scatter.4.cloned.1.call-update
  9.4 0.0 all-gather.6.cloned.1.call-start
  9.4 39.6 %reduce-scatter.6.cloned.1.call-done = bf16[2,64,1024]{2,1,0:T(8,128)(2,1)} async-done(((bf16[2,512,1024]{2,1,0:T(8,128)(2,1)}), bf16[2,64,1024]{2,1,0:T(8,128)(2,1)}) %reduce-scatter.6.cloned.1.call-update) | async-done | bytes 262160 | tf_op jit(solution)/shard_map/reduce_scatter | solution.py:35
  49.1 0.0 copy-done.4
  49.1 0.0 copy-done.5
  49.1 2.1 fusion.1
  51.2 0.0 all-gather.6.cloned.1.call-update
  51.2 0.0 all-gather.8.cloned.1.call-start
  51.3 48.6 %reduce-scatter.8.cloned.1.call-done = bf16[2,512,256]{2,1,0:T(8,128)(2,1)} async-done(((bf16[2,512,2048]{2,1,0:T(8,128)(2,1)}), bf16[2,512,256]{2,1,0:T(8,128)(2,1)}) %reduce-scatter.8.cloned.1.call-update) | async-done | bytes 524304 | tf_op jit(solution)/shard_map/reduce_scatter | solution.py:41
  99.9 3.6 %fusion = (bf16[2,512,256]{2,1,0:T(8,128)(2,1)}, f32[2,512,256]{2,1,0:T(8,128)}, f32[2,512,256]{2,1,0:T(8,128)}) fusion(f32[2,512,256]{2,1,0:T(8,128)} %param.16, bf16[2,512,256]{2,1,0:T(8,128)(2,1)} %reduce-scatter.8.cloned.1.call-done, f32[2,512,256]{2,1,0:T(8,128)} %param.17), kind=kLoop, calls=%fused_computation.9 | loop fusion | flops 2359296 | bytes 5242880 | tf_op jit(solution)/shard_map/convert_element_type | solution.py:56
  103.5 0.0 all-gather.8.cloned.1.call-update
  103.6 0.0 all-gather.4.cloned.1.call-start
  103.6 66.8 %reduce-scatter.4.cloned.1.call-done = bf16[2,256,768]{2,1,0:T(8,128)(2,1)} async-done(((bf16[2,2048,768]{2,1,0:T(8,128)(2,1)}), bf16[2,256,768]{2,1,0:T(8,128)(2,1)}) %reduce-scatter.4.cloned.1.call-update) | async-done | bytes 786448 | tf_op jit(solution)/shard_map/reduce_scatter | solution.py:29
  170.4 0.0 copy-done.2
  170.4 0.0 copy-done.3
  170.4 3.5 %fusion.2 = (bf16[2,256,768]{2,1,0:T(8,128)(2,1)}, f32[2,256,768]{2,1,0:T(8,128)}, f32[2,256,768]{2,1,0:T(8,128)}) fusion(f32[2,256,768]{2,1,0:T(8,128)S(1)} %copy-done.2, bf16[2,256,768]{2,1,0:T(8,128)(2,1)} %reduce-scatter.4.cloned.1.call-done, f32[2,256,768]{2,1,0:T(8,128)S(1)} %copy-done.3), kind=kLoop, calls=%fused_computation.11 | loop fusion | flops 3538944 | bytes 7864320 | tf_op jit(solution)/shard_map/convert_element_type | solution.py:54
  173.9 0.0 all-gather.4.cloned.1.call-update
  174.0 26.2 %all-gather.6.cloned.1.call-done = bf16[2,512,1024]{2,1,0:T(8,128)(2,1)} async-done(((bf16[2,64,1024]{2,1,0:T(8,128)(2,1)}), bf16[2,512,1024]{2,1,0:T(8,128)(2,1)}) %all-gather.6.cloned.1.call-update) | async-done | bytes 2097168 | tf_op jit(solution)/shard_map/all_gather | solution.py:55
  200.1 49.3 %all-gather.8.cloned.1.call-done = bf16[2,512,2048]{2,1,0:T(8,128)(2,1)} async-done(((bf16[2,512,256]{2,1,0:T(8,128)(2,1)}), bf16[2,512,2048]{2,1,0:T(8,128)(2,1)}) %all-gather.8.cloned.1.call-update) | async-done | bytes 4194320 | tf_op jit(solution)/shard_map/all_gather | solution.py:56
  249.4 64.9 %all-gather.4.cloned.1.call-done = bf16[2,2048,768]{2,1,0:T(8,128)(2,1)} async-done(((bf16[2,256,768]{2,1,0:T(8,128)(2,1)}), bf16[2,2048,768]{2,1,0:T(8,128)(2,1)}) %all-gather.4.cloned.1.call-update) | async-done | bytes 6291472 | tf_op jit(solution)/shard_map/all_gather | solution.py:54
  314.3 6.0 %copy.21 = bf16[2,2048,768]{2,1,0:T(8,128)(2,1)} copy(bf16[2,2048,768]{2,1,0:T(8,128)(2,1)} %all-gather.4.cloned.1.call-done) | data formatting | bytes 12582912
  320.4 0.0 copy-done.1
  320.4 1.3 copy.22
  321.7 1.6 copy-done
  323.3 2.0 copy.23
  (4 shorter events, 0.0 us)
Async XLA Ops:
  7.2 41.9 %reduce-scatter.6.cloned.1.call-start = ((), (), s32[]{:S(2)}) async-start(), calls=%async_computation.5 | async-start | bytes 2359296 | tf_op jit(solution)/shard_map/reduce_scatter | solution.py:35
  7.9 92.0 %reduce-scatter.8.cloned.1.call-start = ((), (), s32[]{:S(2)}) async-start(), calls=%async_computation.7 | async-start | bytes 4718592 | tf_op jit(solution)/shard_map/reduce_scatter | solution.py:41
  8.7 161.8 %reduce-scatter.4.cloned.1.call-start = ((), (), s32[]{:S(2)}) async-start(), calls=%async_computation.3 | async-start | bytes 7077888 | tf_op jit(solution)/shard_map/reduce_scatter | solution.py:29
  8.7 40.4 %copy-start.4 = (f32[2,64,1024]{2,1,0:T(8,128)S(1)}, f32[2,64,1024]{2,1,0:T(8,128)}, u32[]{:S(2)}) copy-start(f32[2,64,1024]{2,1,0:T(8,128)} %param.13) | copy-start | bytes 1572868
  8.7 40.3 %copy-start.5 = (f32[2,64,1024]{2,1,0:T(8,128)S(1)}, f32[2,64,1024]{2,1,0:T(8,128)}, u32[]{:S(2)}) copy-start(f32[2,64,1024]{2,1,0:T(8,128)} %param.14) | copy-start | bytes 1572868
  9.4 190.7 %all-gather.6.cloned.1.call-start = ((), (), s32[]{:S(2)}) async-start(), calls=%async_computation.6 | async-start | bytes 2359296 | tf_op jit(solution)/shard_map/all_gather | solution.py:55
  51.2 198.2 %all-gather.8.cloned.1.call-start = ((), (), s32[]{:S(2)}) async-start(), calls=%async_computation.8 | async-start | bytes 4718592 | tf_op jit(solution)/shard_map/all_gather | solution.py:56
  99.9 70.5 %copy-start.2 = (f32[2,256,768]{2,1,0:T(8,128)S(1)}, f32[2,256,768]{2,1,0:T(8,128)}, u32[]{:S(2)}) copy-start(f32[2,256,768]{2,1,0:T(8,128)} %param.10) | copy-start | bytes 4718596
  99.9 70.5 %copy-start.3 = (f32[2,256,768]{2,1,0:T(8,128)S(1)}, f32[2,256,768]{2,1,0:T(8,128)}, u32[]{:S(2)}) copy-start(f32[2,256,768]{2,1,0:T(8,128)} %param.11) | copy-start | bytes 4718596
  103.6 210.8 %all-gather.4.cloned.1.call-start = ((), (), s32[]{:S(2)}) async-start(), calls=%async_computation.4 | async-start | bytes 7077888 | tf_op jit(solution)/shard_map/all_gather | solution.py:54
  314.3 6.0 %copy-start.1 = (bf16[2,512,1024]{2,1,0:T(8,128)(2,1)S(1)}, bf16[2,512,1024]{2,1,0:T(8,128)(2,1)}, u32[]{:S(2)}) copy-start(bf16[2,512,1024]{2,1,0:T(8,128)(2,1)} %all-gather.6.cloned.1.call-done) | copy-start | bytes 6291460
  320.4 2.9 copy-start
Sparse Core Ops, SparseCore 0:
  10.3 38.7 reduce-scatter.5
  51.3 48.5 reduce-scatter.7
  102.2 68.1 reduce-scatter.3
  172.5 27.6 all-gather.5
  202.1 47.1 all-gather.7
  251.4 62.8 all-gather.3
where the time goes:
time: 332 us
  waiting for transfers between devices  298 us (90%)
  between operations  14.1 us (4%)
  local copies, waits for them, and re-layouts  11 us (3%)
  other arithmetic  9.27 us (3%)
    reduce_scatter x1, waiting for transfers between devices, outer_step(): lax.psum_scatter(delta_query[0].astype(jnp.float32).astype(jnp.bfloat16),...  66.8 us
    all_gather x1, waiting for transfers between devices, outer_step(): lax.all_gather(query_master.astype(jnp.bfloat16), 'rep', axis=1, tiled=True)  64.9 us
    all_gather x1, waiting for transfers between devices, outer_step(): lax.all_gather(output_master.astype(jnp.bfloat16), 'rep', axis=2, tiled=T...  49.3 us
    reduce_scatter x1, waiting for transfers between devices, outer_step(): lax.psum_scatter(delta_output[0].astype(jnp.float32).astype(jnp.bfloat16)...  48.6 us
    reduce_scatter x1, waiting for transfers between devices, outer_step(): lax.psum_scatter(delta_latent[0].astype(jnp.float32).astype(jnp.bfloat16)...  39.6 us
    all_gather x1, waiting for transfers between devices, outer_step(): lax.all_gather(latent_master.astype(jnp.bfloat16), 'rep', axis=1, tiled=T...  26.2 us
    unnamed x15, local copies, waits for them, and re-layouts  11 us
  transfers between devices with their start and end apart: 6, of which 6 were waited for; matrix products, arithmetic and copies ran while one was open for 3% of the time, Pallas kernels for 0%

commit v1 on v0

v1 whole, which is shorter than its diff:
```python
import functools

import jax
import jax.numpy as jnp
from jax import lax
from jax.experimental import pallas as pl
from jax.experimental.pallas import tpu as pltpu
from jax.sharding import PartitionSpec as P


OUTER_RATE = 0.7
OUTER_MOMENTUM = 0.9
CORES = 2


def nesterov(totals, master, moment, replica_count):
    average = totals / replica_count
    momentum = OUTER_MOMENTUM * moment + average
    updated = master - OUTER_RATE * (average + OUTER_MOMENTUM * momentum)
    return (updated, momentum)


def pack_body(place, kept_in, sent_in, kept, sent):
    kept[0] = kept_in[...]
    sent[0] = sent_in[...]


def pack(place, delta, axis, chips, first, count):
    chunk = list(delta.shape)
    chunk[0] = count
    chunk[axis] //= chips * CORES

    def source(flip):
        def index(step, place):
            core = place[1] if not flip else 1 - place[1]
            where = [first // count, 0, 0]
            where[axis] = ((place[0] + step) % chips) * CORES + core
            return tuple(where)

        return index

    shape = jax.ShapeDtypeStruct((chips, *chunk), delta.dtype)
    out = pl.BlockSpec((1, *chunk), lambda step, place: (step, 0, 0, 0))
    return pl.pallas_call(
        pack_body,
        grid_spec=pltpu.PrefetchScalarGridSpec(
            num_scalar_prefetch=1,
            grid=(chips,),
            in_specs=[
                pl.BlockSpec(tuple(chunk), source(False)),
                pl.BlockSpec(tuple(chunk), source(True)),
            ],
            out_specs=[out, out],
        ),
        out_shape=[shape, shape],
        name="pack",
    )(place, delta, delta)


def place_body(place, *refs, pieces, axis, chips, width):
    sources, whole, stage, loaded, stored = refs[:-4], *refs[-4:]

    def visit(act):
        for k, (distance, flip, layer, layers) in enumerate(pieces):
            chip = place[0] + distance
            core = 1 - place[1] if flip else place[1]
            slot = chip * CORES + core
            where = [pl.ds(layer, layers), slice(None), slice(None)]
            where[axis] = pl.ds(pl.multiple_of(slot * width, width), width)
            held = stage.at[slot, pl.ds(layer, layers)]
            load = pltpu.make_async_copy(sources[k], held, loaded.at[k])
            store = pltpu.make_async_copy(held, whole.at[tuple(where)], stored.at[k])
            pl.when((chip >= 0) & (chip < chips))(functools.partial(act, load, store))

    def forward(load, store):
        load.wait()
        store.start()

    visit(lambda load, store: load.start())
    visit(forward)
    visit(lambda load, store: store.wait())


def assemble(place, arrays, pieces, axis, chips, shape, dtype):
    width = shape[axis]
    full = list(shape)
    full[axis] = width * chips * CORES
    count = len(arrays)
    return pl.pallas_call(
        functools.partial(place_body, pieces=pieces, axis=axis, chips=chips, width=width),
        in_specs=[pl.BlockSpec(memory_space=pltpu.SMEM)]
        + [pl.BlockSpec(memory_space=pl.ANY)] * count,
        out_specs=pl.BlockSpec(memory_space=pl.ANY),
        out_shape=jax.ShapeDtypeStruct(tuple(full), dtype),
        scratch_shapes=[
            pltpu.VMEM((chips * CORES, *shape), dtype),
            pltpu.SemaphoreType.DMA((count,)),
            pltpu.SemaphoreType.DMA((count,)),
        ],
        name="assemble",
    )(place, *arrays)


def timetable(names, chips):
    steps = [("reduce", d) for d in range(chips - 1, 0, -1)]
    steps += [("gather", d) for d in range(1, chips)]
    offset = max(1, chips // 2)
    order = []
    for slot in range(len(steps) + offset * len(names)):
        for k, name in enumerate(names):
            at = slot - offset * k
            if 0 <= at < len(steps):
                order.append((name, *steps[at]))
    return order


def outer_step(*args):
    matrices = {
        "query": (*args[0:3], 1),
        "latent": (*args[3:6], 1),
        "output": (*args[6:9], 2),
    }
    replicas = lax.axis_size("rep")
    chips = replicas // CORES
    me = lax.axis_index("rep")
    place = jnp.stack([me // CORES, me % CORES]).astype(jnp.int32)
    f32, bf16 = jnp.float32, jnp.bfloat16
    layers = args[0].shape[1]
    groups = {"output": ("output", 0, layers)}
    groups.update({f"query{n}": ("query", n, 1) for n in range(layers)})
    groups["latent"] = ("latent", 0, layers)

    def to_chip(x, step, senders):
        pairs = [
            (q * CORES + c, (q + step) * CORES + c) for q in senders for c in range(CORES)
        ]
        return lax.ppermute(x, "rep", pairs)

    def to_core(x):
        return lax.ppermute(x, "rep", [(r, r ^ 1) for r in range(replicas)])

    kept, got = {}, {}
    for name, (matrix, first, count) in groups.items():
        delta, _, _, axis = matrices[matrix]
        kept[name], sent = pack(place, delta[0], axis, chips, first, count)
        got[name] = to_core(sent)

    def pair_sum(name, distance):
        d = distance % chips
        return kept[name][d].astype(f32) + got[name][d].astype(f32)

    right, left, totals = {}, {}, {}
    pieces = {matrix: [] for matrix in matrices}
    arrays = {matrix: [] for matrix in matrices}

    def keep_piece(name, piece, distance):
        matrix, first, count = groups[name]
        for flip, held in ((False, piece), (True, to_core(piece))):
            arrays[matrix].append(held)
            pieces[matrix].append((distance, flip, first, count))

    for name, kind, d in timetable(list(groups), chips):
        matrix, first, count = groups[name]
        if kind == "reduce":
            a, b = pair_sum(name, d), pair_sum(name, -d)
            if name in right:
                a, b = a + right[name].astype(f32), b + left[name].astype(f32)
            a, b = a.astype(bf16), b.astype(bf16)
            senders = range(chips - d)
        else:
            if d == 1:
                _, master, moment, _ = matrices[matrix]
                total = pair_sum(name, 0)
                if name in right:
                    total = total + right[name].astype(f32) + left[name].astype(f32)
                totals[name] = total
                span = slice(first, first + count)
                updated, _ = nesterov(total, master[span], moment[span], replicas)
                right[name] = left[name] = updated.astype(bf16)
                keep_piece(name, right[name], 0)
            a, b = right[name], left[name]
            senders = range(d - 1, chips - 1)
        right[name] = to_chip(a, 1, senders)
        left[name] = to_chip(b, -1, [chips - 1 - q for q in senders])
        if kind == "gather":
            keep_piece(name, right[name], -d)
            keep_piece(name, left[name], d)

    results = []
    for matrix, (delta, master, moment, axis) in matrices.items():
        parts = [totals[name] for name in groups if groups[name][0] == matrix]
        total = parts[0] if len(parts) == 1 else jnp.concatenate(parts)
        params = assemble(
            place, arrays[matrix], pieces[matrix], axis, chips, master.shape, bf16
        )
        results += [params, *nesterov(total, master, moment, replicas)]
    return tuple(results)


def solution(mesh):
    rows = P(None, "rep", "tp")
    cols = P(None, "tp", "rep")
    by_rows = (P("rep", None, None, "tp"), rows, rows)
    by_cols = (P("rep", None, "tp", None), cols, cols)
    return jax.shard_map(
        outer_step,
        mesh=mesh,
        in_specs=by_rows + by_rows + by_cols,
        out_specs=(
            (P(None, None, "tp"), rows, rows)
            + (P(None, None, "tp"), rows, rows)
            + (P(None, "tp", None), cols, cols)
        ),
        check_vma=False,
    )
```

time: 332 us -> 292 us (0.88)
  waiting for transfers between devices: 298 us -> 122 us
  starting transfers between devices: 0.24 us -> 111 us
  Pallas kernels: 0 us -> 33.4 us
  between operations: 14.1 us -> 2.35 us
  other arithmetic: 9.27 us -> 19.7 us
  local copies, waits for them, and re-layouts: 11 us -> 2.3 us
    reduce_scatter x3 -> x0, waiting for transfers between devices: 155 us -> none  [the longest x1 66.8 us: outer_step(): lax.psum_scatter(delta_query[0].astype(jnp.float32).astype(jnp.bfloat16),...]
    all_gather x3 -> x0, waiting for transfers between devices: 140 us -> none  [the longest x1 64.9 us: outer_step(): lax.all_gather(query_master.astype(jnp.bfloat16), 'rep', axis=1, tiled=True)]
    ppermute x0 -> x80, waiting for transfers between devices: none -> 122 us  [the longest x48 120 us: to_chip(): return lax.ppermute(x, 'rep', pairs)]
    ppermute x0 -> x80, starting transfers between devices: none -> 111 us  [the longest x48 105 us: to_chip(): return lax.ppermute(x, 'rep', pairs)]
    pallas_call x0 -> x7, Pallas kernels: none -> 33.4 us  [the longest x4 19.5 us: pack(): pl.pallas_call(pack_body, grid_spec=pltpu.PrefetchScalarGridSpec(num_scal...]
    unnamed x15 -> x118, local copies, waits for them, and re-layouts: 11 us -> 2.3 us
    convert_element_type x3 -> x19, other arithmetic: 9.27 us -> 15.6 us  [the longest x16 8.7 us: outer_step(): a, b = (a.astype(bf16), b.astype(bf16))]
    sub x0 -> x1, other arithmetic: none -> 3.44 us  [nesterov(): updated = master - OUTER_RATE * (average + OUTER_MOMENTUM * momentum)]
  transfers between devices with their start and end apart: 6 -> 80, of which waited for: 6 -> 23; matrix products, arithmetic and copies ran while one was open for 3% -> 7% of each run, Pallas kernels for 0% -> 8%
where the time goes in v1:
time: 292 us; the launch traced here: 291 us
  waiting for transfers between devices  122 us (42%)
  starting transfers between devices  111 us (38%)
  Pallas kernels  33.4 us (11%)
  other arithmetic  19.7 us (7%)
    ppermute x48, waiting for transfers between devices, to_chip(): return lax.ppermute(x, 'rep', pairs)  120 us
    ppermute x48, starting transfers between devices, to_chip(): return lax.ppermute(x, 'rep', pairs)  105 us
    pallas_call x4, Pallas kernels, pack(): pl.pallas_call(pack_body, grid_spec=pltpu.PrefetchScalarGridSpec(num_scal...  19.5 us
    pallas_call x3, Pallas kernels, assemble(): pl.pallas_call(functools.partial(place_body, pieces=pieces, axis=axis, ch...  13.9 us
    convert_element_type x16, other arithmetic, outer_step(): a, b = (a.astype(bf16), b.astype(bf16))  8.7 us
    convert_element_type x3, other arithmetic, outer_step(): right[name] = left[name] = updated.astype(bf16)  6.93 us
    ppermute x32, starting transfers between devices, to_core(): return lax.ppermute(x, 'rep', [(r, r ^ 1) for r in range(replicas)])  6.6 us
  transfers between devices with their start and end apart: 80, of which 23 were waited for; matrix products, arithmetic and copies ran while one was open for 7% of the time, Pallas kernels for 8%

profile of v1, /device:TPU:0, one launch (start us, length us, event | category | flops | bytes accessed | tf_op | source)
XLA Modules:
  0.0 290.6 jit_solution(6886704038382541623)
XLA Ops:
  1.3 4.4 %pack.6 = (bf16[4,2,64,1024]{3,2,1,0:T(8,128)(2,1)}, bf16[4,2,64,1024]{3,2,1,0:T(8,128)(2,1)}) custom-call(s32[2]{0:T(128)} %pad_add_fusion.place, bf16[2,512,1024]{2,1,0:T(8,128)(2,1)} %bitcast.113, bf16[2,512,1024]{2,1,0:T(8,128)(2,1)} %bitcast.114), custom_call_target="tpu_custom_call" | custom-call | tf_op jit(solution)/shard_map/pack/pallas_call | solution.py:44
  6.2 4.8 %pack.5 = (bf16[4,1,256,768]{3,2,1,0:T(8,128)(2,1)}, bf16[4,1,256,768]{3,2,1,0:T(8,128)(2,1)}) custom-call(s32[2]{0:T(128)} %pad_add_fusion.place, bf16[2,2048,768]{2,1,0:T(8,128)(2,1)} %bitcast.107, bf16[2,2048,768]{2,1,0:T(8,128)(2,1)} %bitcast.108), custom_call_target="tpu_custom_call" | custom-call | tf_op jit(solution)/shard_map/pack/pallas_call | solution.py:44
  11.1 4.8 %pack.4 = (bf16[4,1,256,768]{3,2,1,0:T(8,128)(2,1)}, bf16[4,1,256,768]{3,2,1,0:T(8,128)(2,1)}) custom-call(s32[2]{0:T(128)} %pad_add_fusion.place, bf16[2,2048,768]{2,1,0:T(8,128)(2,1)} %bitcast.109, bf16[2,2048,768]{2,1,0:T(8,128)(2,1)} %bitcast.110), custom_call_target="tpu_custom_call" | custom-call | tf_op jit(solution)/shard_map/pack/pallas_call | solution.py:44
  17.8 4.5 %collective-permute-start.41 = (bf16[2,64,1024]{2,1,0:T(8,128)(2,1)S(1)}, bf16[2,64,1024]{2,1,0:T(8,128)(2,1)S(1)}, u32[]{:S(2)}, u32[]{:S(2)}) collective-permute-start(bf16[2,64,1024]{2,1,0:T(8,128)(2,1)S(1)} %get-tuple-element.53), channel_id=1, source_target_pairs={{0,8},{4,12},{1,9},{5,13},{2,10},{6,14},{3,11},{7,15}} | collective-permute-start | bytes 786440 | tf_op jit(solution)/shard_map/ppermute | solution.py:137
  23.7 4.8 %collective-permute-done.41 = bf16[2,64,1024]{2,1,0:T(8,128)(2,1)S(1)} collective-permute-done((bf16[2,64,1024]{2,1,0:T(8,128)(2,1)S(1)}, bf16[2,64,1024]{2,1,0:T(8,128)(2,1)S(1)}, u32[]{:S(2)}, u32[]{:S(2)}) %collective-permute-start.41) | collective-permute-done | bytes 262176 | tf_op jit(solution)/shard_map/ppermute | solution.py:137
  30.3 5.1 %collective-permute-start.42 = (bf16[2,64,1024]{2,1,0:T(8,128)(2,1)}, bf16[2,64,1024]{2,1,0:T(8,128)(2,1)}, u32[]{:S(2)}, u32[]{:S(2)}) collective-permute-start(bf16[2,64,1024]{2,1,0:T(8,128)(2,1)} %fusion.17), channel_id=1, source_target_pairs={{0,8},{4,12},{8,16},{12,20},{1,9},{5,13},{9,17},{13,21},{2,10},{6,... | collective-permute-start | bytes 786440 | tf_op jit(solution)/shard_map/ppermute | solution.py:137
  35.4 5.4 %pack.7 = (bf16[4,2,512,256]{3,2,1,0:T(8,128)(2,1)}, bf16[4,2,512,256]{3,2,1,0:T(8,128)(2,1)}) custom-call(s32[2]{0:T(128)} %pad_add_fusion.place, bf16[2,512,2048]{2,1,0:T(8,128)(2,1)} %bitcast.111, bf16[2,512,2048]{2,1,0:T(8,128)(2,1)} %bitcast.112), custom_call_target="tpu_custom_call" | custom-call | tf_op jit(solution)/shard_map/pack/pallas_call | solution.py:44
  42.6 4.0 %collective-permute-start.43 = (bf16[2,64,1024]{2,1,0:T(8,128)(2,1)S(1)}, bf16[2,64,1024]{2,1,0:T(8,128)(2,1)S(1)}, u32[]{:S(2)}, u32[]{:S(2)}) collective-permute-start(bf16[2,64,1024]{2,1,0:T(8,128)(2,1)S(1)} %get-tuple-element.51), channel_id=1, source_target_pairs={{0,8},{4,12},{8,16},{12,20},{16,24},{20,28},{1,9},{5,13},{9,17},{1... | collective-permute-start | bytes 786440 | tf_op jit(solution)/shard_map/ppermute | solution.py:137
  51.4 6.3 %collective-permute-start.1 = (bf16[1,256,768]{2,1,0:T(8,128)(2,1)S(1)}, bf16[1,256,768]{2,1,0:T(8,128)(2,1)S(1)}, u32[]{:S(2)}, u32[]{:S(2)}) collective-permute-start(bf16[1,256,768]{2,1,0:T(8,128)(2,1)S(1)} %get-tuple-element.49), channel_id=1, source_target_pairs={{0,8},{4,12},{1,9},{5,13},{2,10},{6,14},{3,11},{7,15}} | collective-permute-start | bytes 1179656 | tf_op jit(solution)/shard_map/ppermute | solution.py:137
  62.7 5.2 %collective-permute-done.1 = bf16[1,256,768]{2,1,0:T(8,128)(2,1)S(1)} collective-permute-done((bf16[1,256,768]{2,1,0:T(8,128)(2,1)S(1)}, bf16[1,256,768]{2,1,0:T(8,128)(2,1)S(1)}, u32[]{:S(2)}, u32[]{:S(2)}) %collective-permute-start.1) | collective-permute-done | bytes 393248 | tf_op jit(solution)/shard_map/ppermute | solution.py:137
  67.9 4.4 %collective-permute-start.22 = (bf16[1,256,768]{2,1,0:T(8,128)(2,1)S(1)}, bf16[1,256,768]{2,1,0:T(8,128)(2,1)S(1)}, u32[]{:S(2)}, u32[]{:S(2)}) collective-permute-start(bf16[1,256,768]{2,1,0:T(8,128)(2,1)S(1)} %fusion.7), channel_id=1, source_target_pairs={{0,8},{4,12},{8,16},{12,20},{1,9},{5,13},{9,17},{13,21},{2,10},{6,... | collective-permute-start | bytes 1179656 | tf_op jit(solution)/shard_map/ppermute | solution.py:137
  81.8 4.4 %collective-permute-start.48 = (bf16[2,64,1024]{2,1,0:T(8,128)(2,1)S(1)}, bf16[2,64,1024]{2,1,0:T(8,128)(2,1)S(1)}, u32[]{:S(2)}, u32[]{:S(2)}) collective-permute-start(bf16[2,64,1024]{2,1,0:T(8,128)(2,1)S(1)} %get-tuple-element.28.refs_0_), channel_id=1, source_target_pairs={{0,8},{4,12},{8,16},{12,20},{16,24},{20,28},{1,9},{5,13},{9,17},{1... | collective-permute-start | bytes 786440 | tf_op jit(solution)/shard_map/ppermute | solution.py:137
  86.5 3.6 %collective-permute-done.2 = bf16[1,256,768]{2,1,0:T(8,128)(2,1)S(1)} collective-permute-done((bf16[1,256,768]{2,1,0:T(8,128)(2,1)S(1)}, bf16[1,256,768]{2,1,0:T(8,128)(2,1)S(1)}, u32[]{:S(2)}, u32[]{:S(2)}) %collective-permute-start.2) | collective-permute-done | bytes 393248 | tf_op jit(solution)/shard_map/ppermute | solution.py:137
  92.3 5.8 %collective-permute-start.61 = (bf16[2,512,256]{2,1,0:T(8,128)(2,1)S(1)}, bf16[2,512,256]{2,1,0:T(8,128)(2,1)S(1)}, u32[]{:S(2)}, u32[]{:S(2)}) collective-permute-start(bf16[2,512,256]{2,1,0:T(8,128)(2,1)S(1)} %get-tuple-element.39), channel_id=1, source_target_pairs={{0,8},{4,12},{1,9},{5,13},{2,10},{6,14},{3,11},{7,15}} | collective-permute-start | bytes 1572872 | tf_op jit(solution)/shard_map/ppermute | solution.py:137
  100.5 12.4 %collective-permute-done.54.refs_8_ = bf16[2,64,1024]{2,1,0:T(8,128)(2,1)S(1)} collective-permute-done((bf16[2,64,1024]{2,1,0:T(8,128)(2,1)S(1)}, bf16[2,64,1024]{2,1,0:T(8,128)(2,1)S(1)}, u32[]{:S(2)}, u32[]{:S(2)}) %collective-permute-start.54) | collective-permute-done | bytes 262176 | tf_op jit(solution)/shard_map/ppermute | solution.py:137
  113.9 4.7 %collective-permute-start.23 = (bf16[1,256,768]{2,1,0:T(8,128)(2,1)S(1)}, bf16[1,256,768]{2,1,0:T(8,128)(2,1)S(1)}, u32[]{:S(2)}, u32[]{:S(2)}) collective-permute-start(bf16[1,256,768]{2,1,0:T(8,128)(2,1)S(1)} %get-tuple-element.43), channel_id=1, source_target_pairs={{0,8},{4,12},{8,16},{12,20},{16,24},{20,28},{1,9},{5,13},{9,17},{1... | collective-permute-start | bytes 1179656 | tf_op jit(solution)/shard_map/ppermute | solution.py:137
  118.6 4.6 %collective-permute-start.3 = (bf16[1,256,768]{2,1,0:T(8,128)(2,1)S(1)}, bf16[1,256,768]{2,1,0:T(8,128)(2,1)S(1)}, u32[]{:S(2)}, u32[]{:S(2)}) collective-permute-start(bf16[1,256,768]{2,1,0:T(8,128)(2,1)S(1)} %get-tuple-element.47), channel_id=1, source_target_pairs={{0,8},{4,12},{8,16},{12,20},{16,24},{20,28},{1,9},{5,13},{9,17},{1... | collective-permute-start | bytes 1179656 | tf_op jit(solution)/shard_map/ppermute | solution.py:137
  126.1 5.7 %collective-permute-start.62 = (bf16[2,512,256]{2,1,0:T(8,128)(2,1)S(1)}, bf16[2,512,256]{2,1,0:T(8,128)(2,1)S(1)}, u32[]{:S(2)}, u32[]{:S(2)}) collective-permute-start(bf16[2,512,256]{2,1,0:T(8,128)(2,1)S(1)} %fusion.1), channel_id=1, source_target_pairs={{0,8},{4,12},{8,16},{12,20},{1,9},{5,13},{9,17},{13,21},{2,10},{6,... | collective-permute-start | bytes 1572872 | tf_op jit(solution)/shard_map/ppermute | solution.py:137
  138.3 7.8 %collective-permute-done.6 = bf16[1,256,768]{2,1,0:T(8,128)(2,1)S(1)} collective-permute-done((bf16[1,256,768]{2,1,0:T(8,128)(2,1)S(1)}, bf16[1,256,768]{2,1,0:T(8,128)(2,1)S(1)}, u32[]{:S(2)}, u32[]{:S(2)}) %collective-permute-start.6) | collective-permute-done | bytes 393248 | tf_op jit(solution)/shard_map/ppermute | solution.py:137
  151.6 4.6 %collective-permute-start.28 = (bf16[1,256,768]{2,1,0:T(8,128)(2,1)S(1)}, bf16[1,256,768]{2,1,0:T(8,128)(2,1)S(1)}, u32[]{:S(2)}, u32[]{:S(2)}) collective-permute-start(bf16[1,256,768]{2,1,0:T(8,128)(2,1)S(1)} %get-tuple-element.33.refs_14_), channel_id=1, source_target_pairs={{0,8},{4,12},{8,16},{12,20},{16,24},{20,28},{1,9},{5,13},{9,17},{1... | collective-permute-start | bytes 1179656 | tf_op jit(solution)/shard_map/ppermute | solution.py:137
  159.5 3.9 %collective-permute-done.30.refs_18_ = bf16[1,256,768]{2,1,0:T(8,128)(2,1)S(1)} collective-permute-done((bf16[1,256,768]{2,1,0:T(8,128)(2,1)S(1)}, bf16[1,256,768]{2,1,0:T(8,128)(2,1)S(1)}, u32[]{:S(2)}, u32[]{:S(2)}) %collective-permute-start.30) | collective-permute-done | bytes 393248 | tf_op jit(solution)/shard_map/ppermute | solution.py:137
  166.9 3.6 %collective-permute-start.63 = (bf16[2,512,256]{2,1,0:T(8,128)(2,1)S(1)}, bf16[2,512,256]{2,1,0:T(8,128)(2,1)S(1)}, u32[]{:S(2)}, u32[]{:S(2)}) collective-permute-start(bf16[2,512,256]{2,1,0:T(8,128)(2,1)S(1)} %get-tuple-element.37), channel_id=1, source_target_pairs={{0,8},{4,12},{8,16},{12,20},{16,24},{20,28},{1,9},{5,13},{9,17},{1... | collective-permute-start | bytes 1572872 | tf_op jit(solution)/shard_map/ppermute | solution.py:137
  176.9 7.8 %collective-permute-done.63 = bf16[2,512,256]{2,1,0:T(8,128)(2,1)S(1)} collective-permute-done((bf16[2,512,256]{2,1,0:T(8,128)(2,1)S(1)}, bf16[2,512,256]{2,1,0:T(8,128)(2,1)S(1)}, u32[]{:S(2)}, u32[]{:S(2)}) %collective-permute-start.63) | collective-permute-done | bytes 524320 | tf_op jit(solution)/shard_map/ppermute | solution.py:137
  186.0 9.0 %collective-permute-done.34.refs_22_ = bf16[1,256,768]{2,1,0:T(8,128)(2,1)S(1)} collective-permute-done((bf16[1,256,768]{2,1,0:T(8,128)(2,1)S(1)}, bf16[1,256,768]{2,1,0:T(8,128)(2,1)S(1)}, u32[]{:S(2)}, u32[]{:S(2)}) %collective-permute-start.34) | collective-permute-done | bytes 393248 | tf_op jit(solution)/shard_map/ppermute | solution.py:137
  197.7 15.9 %collective-permute-done.14.refs_8_ = bf16[1,256,768]{2,1,0:T(8,128)(2,1)S(1)} collective-permute-done((bf16[1,256,768]{2,1,0:T(8,128)(2,1)S(1)}, bf16[1,256,768]{2,1,0:T(8,128)(2,1)S(1)}, u32[]{:S(2)}, u32[]{:S(2)}) %collective-permute-start.14) | collective-permute-done | bytes 393248 | tf_op jit(solution)/shard_map/ppermute | solution.py:137
  219.9 7.6 %collective-permute-done.38.refs_26_ = bf16[1,256,768]{2,1,0:T(8,128)(2,1)S(1)} collective-permute-done((bf16[1,256,768]{2,1,0:T(8,128)(2,1)S(1)}, bf16[1,256,768]{2,1,0:T(8,128)(2,1)S(1)}, u32[]{:S(2)}, u32[]{:S(2)}) %collective-permute-start.38) | collective-permute-done | bytes 393248 | tf_op jit(solution)/shard_map/ppermute | solution.py:137
  228.8 5.4 %collective-permute-start.68 = (bf16[2,512,256]{2,1,0:T(8,128)(2,1)S(1)}, bf16[2,512,256]{2,1,0:T(8,128)(2,1)}, u32[]{:S(2)}, u32[]{:S(2)}) collective-permute-start(bf16[2,512,256]{2,1,0:T(8,128)(2,1)S(1)} %get-tuple-element.25.refs_0_), channel_id=1, source_target_pairs={{0,8},{4,12},{8,16},{12,20},{16,24},{20,28},{1,9},{5,13},{9,17},{1... | collective-permute-start | bytes 1572872 | tf_op jit(solution)/shard_map/ppermute | solution.py:137
  236.5 8.7 %collective-permute-done.70.refs_4_ = bf16[2,512,256]{2,1,0:T(8,128)(2,1)S(1)} collective-permute-done((bf16[2,512,256]{2,1,0:T(8,128)(2,1)S(1)}, bf16[2,512,256]{2,1,0:T(8,128)(2,1)S(1)}, u32[]{:S(2)}, u32[]{:S(2)}) %collective-permute-start.70) | collective-permute-done | bytes 524320 | tf_op jit(solution)/shard_map/ppermute | solution.py:137
  248.6 10.5 %collective-permute-done.74.refs_8_ = bf16[2,512,256]{2,1,0:T(8,128)(2,1)} collective-permute-done((bf16[2,512,256]{2,1,0:T(8,128)(2,1)S(1)}, bf16[2,512,256]{2,1,0:T(8,128)(2,1)}, u32[]{:S(2)}, u32[]{:S(2)}) %collective-permute-start.74) | collective-permute-done | bytes 524320 | tf_op jit(solution)/shard_map/ppermute | solution.py:137
  265.1 7.3 %collective-permute-done.78.refs_12_ = bf16[2,512,256]{2,1,0:T(8,128)(2,1)} collective-permute-done((bf16[2,512,256]{2,1,0:T(8,128)(2,1)}, bf16[2,512,256]{2,1,0:T(8,128)(2,1)}, u32[]{:S(2)}, u32[]{:S(2)}) %collective-permute-start.78) | collective-permute-done | bytes 524320 | tf_op jit(solution)/shard_map/ppermute | solution.py:137
  279.7 6.4 %assemble.3 = bf16[2,2048,768]{2,1,0:T(8,128)(2,1)} custom-call(s32[2]{0:T(128)} %pad_add_fusion.place, bf16[1,256,768]{2,1,0:T(8,128)(2,1)} %copy-done.11, bf16[1,256,768]{2,1,0:T(8,128)(2,1)} %copy-done.25, bf16[1,256,768]{2,1,0:T(8,128)(2,1)} %copy-done.24, bf16[1,256,768]{2,1,0:T(8,128)(2,1)} %copy-done.33, bf16[1,256,768]{2,1,0:T(8,128)(2,1)} %copy-done.23, ...), custom_call_target="tpu_custom_call" | custom-call | tf_op jit(solution)/shard_map/assemble/pallas_call | solution.py:89
  286.1 4.4 %assemble.5 = bf16[2,512,2048]{2,1,0:T(8,128)(2,1)} custom-call(s32[2]{0:T(128)} %pad_add_fusion.place, bf16[2,512,256]{2,1,0:T(8,128)(2,1)} %copy-done.9, bf16[2,512,256]{2,1,0:T(8,128)(2,1)} %copy-done.16, bf16[2,512,256]{2,1,0:T(8,128)(2,1)} %collective-permute-done.68.refs_2_, bf16[2,512,256]{2,1,0:T(8,128)(2,1)} %collective-permute-done.69.refs_3_, ...), custom_call_target="tpu_custom_call" | custom-call | tf_op jit(solution)/shard_map/assemble/pallas_call | solution.py:89
  (274 shorter events, 90.7 us)
Async XLA Ops:
  11.0 36.2 %collective-permute-start.20 = (bf16[4,1,256,768]{3,2,1,0:T(8,128)(2,1)}, bf16[4,1,256,768]{3,2,1,0:T(8,128)(2,1)S(1)}, u32[]{:S(2)}, u32[]{:S(2)}) collective-permute-start(bf16[4,1,256,768]{3,2,1,0:T(8,128)(2,1)} %get-tuple-element.20), channel_id=1, source_target_pairs={{0,4},{4,0},{8,12},{12,8},{16,20},{20,16},{24,28},{28,24},{1,5},{5... | collective-permute-start | bytes 4718600 | tf_op jit(solution)/shard_map/ppermute | solution.py:140
  15.9 34.5 %collective-permute-start = (bf16[4,1,256,768]{3,2,1,0:T(8,128)(2,1)}, bf16[4,1,256,768]{3,2,1,0:T(8,128)(2,1)S(1)}, u32[]{:S(2)}, u32[]{:S(2)}) collective-permute-start(bf16[4,1,256,768]{3,2,1,0:T(8,128)(2,1)} %get-tuple-element.18), channel_id=1, source_target_pairs={{0,4},{4,0},{8,12},{12,8},{16,20},{20,16},{24,28},{28,24},{1,5},{5... | collective-permute-start | bytes 4718600 | tf_op jit(solution)/shard_map/ppermute | solution.py:140
  22.3 18.5 %collective-permute-start.44 = (bf16[2,64,1024]{2,1,0:T(8,128)(2,1)S(1)}, bf16[2,64,1024]{2,1,0:T(8,128)(2,1)}, u32[]{:S(2)}, u32[]{:S(2)}) collective-permute-start(bf16[2,64,1024]{2,1,0:T(8,128)(2,1)S(1)} %get-tuple-element.54), channel_id=1, source_target_pairs={{24,16},{28,20},{25,17},{29,21},{26,18},{30,22},{27,19},{31,23}} | collective-permute-start | bytes 786440 | tf_op jit(solution)/shard_map/ppermute | solution.py:137
  40.8 50.5 %collective-permute-start.60 = (bf16[4,2,512,256]{3,2,1,0:T(8,128)(2,1)}, bf16[4,2,512,256]{3,2,1,0:T(8,128)(2,1)S(1)}, u32[]{:S(2)}, u32[]{:S(2)}) collective-permute-start(bf16[4,2,512,256]{3,2,1,0:T(8,128)(2,1)} %get-tuple-element.24), channel_id=1, source_target_pairs={{0,4},{4,0},{8,12},{12,8},{16,20},{20,16},{24,28},{28,24},{1,5},{5... | collective-permute-start | bytes 6291464 | tf_op jit(solution)/shard_map/ppermute | solution.py:140
  42.6 29.9 %collective-permute-start.43 = (bf16[2,64,1024]{2,1,0:T(8,128)(2,1)S(1)}, bf16[2,64,1024]{2,1,0:T(8,128)(2,1)S(1)}, u32[]{:S(2)}, u32[]{:S(2)}) collective-permute-start(bf16[2,64,1024]{2,1,0:T(8,128)(2,1)S(1)} %get-tuple-element.51), channel_id=1, source_target_pairs={{0,8},{4,12},{8,16},{12,20},{16,24},{20,28},{1,9},{5,13},{9,17},{1... | collective-permute-start | bytes 786440 | tf_op jit(solution)/shard_map/ppermute | solution.py:137
  50.5 26.8 %collective-permute-start.24 = (bf16[1,256,768]{2,1,0:T(8,128)(2,1)S(1)}, bf16[1,256,768]{2,1,0:T(8,128)(2,1)S(1)}, u32[]{:S(2)}, u32[]{:S(2)}) collective-permute-start(bf16[1,256,768]{2,1,0:T(8,128)(2,1)S(1)} %get-tuple-element.46), channel_id=1, source_target_pairs={{24,16},{28,20},{25,17},{29,21},{26,18},{30,22},{27,19},{31,23}} | collective-permute-start | bytes 1179656 | tf_op jit(solution)/shard_map/ppermute | solution.py:137
  81.8 17.8 %collective-permute-start.48 = (bf16[2,64,1024]{2,1,0:T(8,128)(2,1)S(1)}, bf16[2,64,1024]{2,1,0:T(8,128)(2,1)S(1)}, u32[]{:S(2)}, u32[]{:S(2)}) collective-permute-start(bf16[2,64,1024]{2,1,0:T(8,128)(2,1)S(1)} %get-tuple-element.28.refs_0_), channel_id=1, source_target_pairs={{0,8},{4,12},{8,16},{12,20},{16,24},{20,28},{1,9},{5,13},{9,17},{1... | collective-permute-start | bytes 786440 | tf_op jit(solution)/shard_map/ppermute | solution.py:137
  91.3 22.3 %collective-permute-start.5 = (bf16[1,256,768]{2,1,0:T(8,128)(2,1)S(1)}, bf16[1,256,768]{2,1,0:T(8,128)(2,1)S(1)}, u32[]{:S(2)}, u32[]{:S(2)}) collective-permute-start(bf16[1,256,768]{2,1,0:T(8,128)(2,1)S(1)} %get-tuple-element.48), channel_id=1, source_target_pairs={{24,16},{28,20},{16,8},{20,12},{25,17},{29,21},{17,9},{21,13},{26,... | collective-permute-start | bytes 1179656 | tf_op jit(solution)/shard_map/ppermute | solution.py:137
  92.3 32.3 %collective-permute-start.61 = (bf16[2,512,256]{2,1,0:T(8,128)(2,1)S(1)}, bf16[2,512,256]{2,1,0:T(8,128)(2,1)S(1)}, u32[]{:S(2)}, u32[]{:S(2)}) collective-permute-start(bf16[2,512,256]{2,1,0:T(8,128)(2,1)S(1)} %get-tuple-element.39), channel_id=1, source_target_pairs={{0,8},{4,12},{1,9},{5,13},{2,10},{6,14},{3,11},{7,15}} | collective-permute-start | bytes 1572872 | tf_op jit(solution)/shard_map/ppermute | solution.py:137
  99.6 26.5 %collective-permute-start.64 = (bf16[2,512,256]{2,1,0:T(8,128)(2,1)S(1)}, bf16[2,512,256]{2,1,0:T(8,128)(2,1)S(1)}, u32[]{:S(2)}, u32[]{:S(2)}) collective-permute-start(bf16[2,512,256]{2,1,0:T(8,128)(2,1)S(1)} %get-tuple-element.40), channel_id=1, source_target_pairs={{24,16},{28,20},{25,17},{29,21},{26,18},{30,22},{27,19},{31,23}} | collective-permute-start | bytes 1572872 | tf_op jit(solution)/shard_map/ppermute | solution.py:137
  113.9 17.9 %collective-permute-start.23 = (bf16[1,256,768]{2,1,0:T(8,128)(2,1)S(1)}, bf16[1,256,768]{2,1,0:T(8,128)(2,1)S(1)}, u32[]{:S(2)}, u32[]{:S(2)}) collective-permute-start(bf16[1,256,768]{2,1,0:T(8,128)(2,1)S(1)} %get-tuple-element.43), channel_id=1, source_target_pairs={{0,8},{4,12},{8,16},{12,20},{16,24},{20,28},{1,9},{5,13},{9,17},{1... | collective-permute-start | bytes 1179656 | tf_op jit(solution)/shard_map/ppermute | solution.py:137
  118.6 17.9 %collective-permute-start.3 = (bf16[1,256,768]{2,1,0:T(8,128)(2,1)S(1)}, bf16[1,256,768]{2,1,0:T(8,128)(2,1)S(1)}, u32[]{:S(2)}, u32[]{:S(2)}) collective-permute-start(bf16[1,256,768]{2,1,0:T(8,128)(2,1)S(1)} %get-tuple-element.47), channel_id=1, source_target_pairs={{0,8},{4,12},{8,16},{12,20},{16,24},{20,28},{1,9},{5,13},{9,17},{1... | collective-permute-start | bytes 1179656 | tf_op jit(solution)/shard_map/ppermute | solution.py:137
  124.6 21.4 %collective-permute-start.6 = (bf16[1,256,768]{2,1,0:T(8,128)(2,1)S(1)}, bf16[1,256,768]{2,1,0:T(8,128)(2,1)S(1)}, u32[]{:S(2)}, u32[]{:S(2)}) collective-permute-start(bf16[1,256,768]{2,1,0:T(8,128)(2,1)S(1)} %fusion.11), channel_id=1, source_target_pairs={{24,16},{28,20},{16,8},{20,12},{8,0},{12,4},{25,17},{29,21},{17,9}... | collective-permute-start | bytes 1179656 | tf_op jit(solution)/shard_map/ppermute | solution.py:137
  126.1 30.0 %collective-permute-start.62 = (bf16[2,512,256]{2,1,0:T(8,128)(2,1)S(1)}, bf16[2,512,256]{2,1,0:T(8,128)(2,1)S(1)}, u32[]{:S(2)}, u32[]{:S(2)}) collective-permute-start(bf16[2,512,256]{2,1,0:T(8,128)(2,1)S(1)} %fusion.1), channel_id=1, source_target_pairs={{0,8},{4,12},{8,16},{12,20},{1,9},{5,13},{9,17},{13,21},{2,10},{6,... | collective-permute-start | bytes 1572872 | tf_op jit(solution)/shard_map/ppermute | solution.py:137
  131.8 18.0 %collective-permute-start.58 = (bf16[2,64,1024]{2,1,0:T(8,128)(2,1)S(1)}, bf16[2,64,1024]{2,1,0:T(8,128)(2,1)S(1)}, u32[]{:S(2)}, u32[]{:S(2)}) collective-permute-start(bf16[2,64,1024]{2,1,0:T(8,128)(2,1)S(1)} %collective-permute-done.54.refs_8_), channel_id=1, source_target_pairs={{8,0},{12,4},{9,1},{13,5},{10,2},{14,6},{11,3},{15,7}} | collective-permute-start | bytes 786440 | tf_op jit(solution)/shard_map/ppermute | solution.py:137
  157.5 18.7 %collective-permute-start.65 = (bf16[2,512,256]{2,1,0:T(8,128)(2,1)S(1)}, bf16[2,512,256]{2,1,0:T(8,128)(2,1)S(1)}, u32[]{:S(2)}, u32[]{:S(2)}) collective-permute-start(bf16[2,512,256]{2,1,0:T(8,128)(2,1)S(1)} %get-tuple-element.38), channel_id=1, source_target_pairs={{24,16},{28,20},{16,8},{20,12},{25,17},{29,21},{17,9},{21,13},{26,... | collective-permute-start | bytes 1572872 | tf_op jit(solution)/shard_map/ppermute | solution.py:137
  166.9 17.8 %collective-permute-start.63 = (bf16[2,512,256]{2,1,0:T(8,128)(2,1)S(1)}, bf16[2,512,256]{2,1,0:T(8,128)(2,1)S(1)}, u32[]{:S(2)}, u32[]{:S(2)}) collective-permute-start(bf16[2,512,256]{2,1,0:T(8,128)(2,1)S(1)} %get-tuple-element.37), channel_id=1, source_target_pairs={{0,8},{4,12},{8,16},{12,20},{16,24},{20,28},{1,9},{5,13},{9,17},{1... | collective-permute-start | bytes 1572872 | tf_op jit(solution)/shard_map/ppermute | solution.py:137
  171.7 23.3 %collective-permute-start.34 = (bf16[1,256,768]{2,1,0:T(8,128)(2,1)S(1)}, bf16[1,256,768]{2,1,0:T(8,128)(2,1)S(1)}, u32[]{:S(2)}, u32[]{:S(2)}) collective-permute-start(bf16[1,256,768]{2,1,0:T(8,128)(2,1)S(1)} %collective-permute-done.30.refs_18_), channel_id=1, source_target_pairs={{16,8},{20,12},{8,0},{12,4},{17,9},{21,13},{9,1},{13,5},{18,10},{2... | collective-permute-start | bytes 1179656 | tf_op jit(solution)/shard_map/ppermute | solution.py:137
  175.5 20.9 %collective-permute-start.31 = (bf16[1,256,768]{2,1,0:T(8,128)(2,1)S(1)}, bf16[1,256,768]{2,1,0:T(8,128)(2,1)S(1)}, u32[]{:S(2)}, u32[]{:S(2)}) collective-permute-start(bf16[1,256,768]{2,1,0:T(8,128)(2,1)S(1)} %collective-permute-done.30.refs_18_), channel_id=1, source_target_pairs={{0,4},{4,0},{8,12},{12,8},{16,20},{20,16},{24,28},{28,24},{1,5},{5... | collective-permute-start | bytes 1179656 | tf_op jit(solution)/shard_map/ppermute | solution.py:140
  175.5 21.0 %collective-permute-start.32 = (bf16[1,256,768]{2,1,0:T(8,128)(2,1)S(1)}, bf16[1,256,768]{2,1,0:T(8,128)(2,1)S(1)}, u32[]{:S(2)}, u32[]{:S(2)}) collective-permute-start(bf16[1,256,768]{2,1,0:T(8,128)(2,1)S(1)} %collective-permute-done.28.refs_16_), channel_id=1, source_target_pairs={{8,16},{12,20},{16,24},{20,28},{9,17},{13,21},{17,25},{21,29},{10,... | collective-permute-start | bytes 1179656 | tf_op jit(solution)/shard_map/ppermute | solution.py:137
  176.2 21.0 %collective-permute-start.29 = (bf16[1,256,768]{2,1,0:T(8,128)(2,1)S(1)}, bf16[1,256,768]{2,1,0:T(8,128)(2,1)S(1)}, u32[]{:S(2)}, u32[]{:S(2)}) collective-permute-start(bf16[1,256,768]{2,1,0:T(8,128)(2,1)S(1)} %collective-permute-done.28.refs_16_), channel_id=1, source_target_pairs={{0,4},{4,0},{8,12},{12,8},{16,20},{20,16},{24,28},{28,24},{1,5},{5... | collective-permute-start | bytes 1179656 | tf_op jit(solution)/shard_map/ppermute | solution.py:140
  184.8 31.5 %collective-permute-start.66 = (bf16[2,512,256]{2,1,0:T(8,128)(2,1)S(1)}, bf16[2,512,256]{2,1,0:T(8,128)(2,1)S(1)}, u32[]{:S(2)}, u32[]{:S(2)}) collective-permute-start(bf16[2,512,256]{2,1,0:T(8,128)(2,1)S(1)} %fusion), channel_id=1, source_target_pairs={{24,16},{28,20},{16,8},{20,12},{8,0},{12,4},{25,17},{29,21},{17,9}... | collective-permute-start | bytes 1572872 | tf_op jit(solution)/shard_map/ppermute | solution.py:137
  195.1 18.5 %collective-permute-start.14 = (bf16[1,256,768]{2,1,0:T(8,128)(2,1)S(1)}, bf16[1,256,768]{2,1,0:T(8,128)(2,1)S(1)}, u32[]{:S(2)}, u32[]{:S(2)}) collective-permute-start(bf16[1,256,768]{2,1,0:T(8,128)(2,1)S(1)} %collective-permute-done.10.refs_4_), channel_id=1, source_target_pairs={{16,8},{20,12},{8,0},{12,4},{17,9},{21,13},{9,1},{13,5},{18,10},{2... | collective-permute-start | bytes 1179656 | tf_op jit(solution)/shard_map/ppermute | solution.py:137
  196.4 18.5 %collective-permute-start.11 = (bf16[1,256,768]{2,1,0:T(8,128)(2,1)S(1)}, bf16[1,256,768]{2,1,0:T(8,128)(2,1)S(1)}, u32[]{:S(2)}, u32[]{:S(2)}) collective-permute-start(bf16[1,256,768]{2,1,0:T(8,128)(2,1)S(1)} %collective-permute-done.10.refs_4_), channel_id=1, source_target_pairs={{0,4},{4,0},{8,12},{12,8},{16,20},{20,16},{24,28},{28,24},{1,5},{5... | collective-permute-start | bytes 1179656 | tf_op jit(solution)/shard_map/ppermute | solution.py:140
  196.5 18.5 %collective-permute-start.12 = (bf16[1,256,768]{2,1,0:T(8,128)(2,1)S(1)}, bf16[1,256,768]{2,1,0:T(8,128)(2,1)S(1)}, u32[]{:S(2)}, u32[]{:S(2)}) collective-permute-start(bf16[1,256,768]{2,1,0:T(8,128)(2,1)S(1)} %collective-permute-done.8.refs_2_), channel_id=1, source_target_pairs={{8,16},{12,20},{16,24},{20,28},{9,17},{13,21},{17,25},{21,29},{10,... | collective-permute-start | bytes 1179656 | tf_op jit(solution)/shard_map/ppermute | solution.py:137
  197.2 18.5 %collective-permute-start.9 = (bf16[1,256,768]{2,1,0:T(8,128)(2,1)S(1)}, bf16[1,256,768]{2,1,0:T(8,128)(2,1)S(1)}, u32[]{:S(2)}, u32[]{:S(2)}) collective-permute-start(bf16[1,256,768]{2,1,0:T(8,128)(2,1)S(1)} %collective-permute-done.8.refs_2_), channel_id=1, source_target_pairs={{0,4},{4,0},{8,12},{12,8},{16,20},{20,16},{24,28},{28,24},{1,5},{5... | collective-permute-start | bytes 1179656 | tf_op jit(solution)/shard_map/ppermute | solution.py:140
  215.0 19.1 %collective-permute-start.36 = (bf16[1,256,768]{2,1,0:T(8,128)(2,1)S(1)}, bf16[1,256,768]{2,1,0:T(8,128)(2,1)S(1)}, u32[]{:S(2)}, u32[]{:S(2)}) collective-permute-start(bf16[1,256,768]{2,1,0:T(8,128)(2,1)S(1)} %collective-permute-done.32.refs_20_), channel_id=1, source_target_pairs={{16,24},{20,28},{17,25},{21,29},{18,26},{22,30},{19,27},{23,31}} | collective-permute-start | bytes 1179656 | tf_op jit(solution)/shard_map/ppermute | solution.py:137
  215.7 18.4 %collective-permute-start.33 = (bf16[1,256,768]{2,1,0:T(8,128)(2,1)S(1)}, bf16[1,256,768]{2,1,0:T(8,128)(2,1)S(1)}, u32[]{:S(2)}, u32[]{:S(2)}) collective-permute-start(bf16[1,256,768]{2,1,0:T(8,128)(2,1)S(1)} %collective-permute-done.32.refs_20_), channel_id=1, source_target_pairs={{0,4},{4,0},{8,12},{12,8},{16,20},{20,16},{24,28},{28,24},{1,5},{5... | collective-permute-start | bytes 1179656 | tf_op jit(solution)/shard_map/ppermute | solution.py:140
  216.5 19.4 %collective-permute-start.18 = (bf16[1,256,768]{2,1,0:T(8,128)(2,1)S(1)}, bf16[1,256,768]{2,1,0:T(8,128)(2,1)S(1)}, u32[]{:S(2)}, u32[]{:S(2)}) collective-permute-start(bf16[1,256,768]{2,1,0:T(8,128)(2,1)S(1)} %collective-permute-done.14.refs_8_), channel_id=1, source_target_pairs={{8,0},{12,4},{9,1},{13,5},{10,2},{14,6},{11,3},{15,7}} | collective-permute-start | bytes 1179656 | tf_op jit(solution)/shard_map/ppermute | solution.py:137
  263.6 22.5 %collective-permute-start.69 = (bf16[2,512,256]{2,1,0:T(8,128)(2,1)}, bf16[2,512,256]{2,1,0:T(8,128)(2,1)}, u32[]{:S(2)}, u32[]{:S(2)}) collective-permute-start(bf16[2,512,256]{2,1,0:T(8,128)(2,1)} %collective-permute-done.68.refs_2_), channel_id=1, source_target_pairs={{0,4},{4,0},{8,12},{12,8},{16,20},{20,16},{24,28},{28,24},{1,5},{5... | collective-permute-start | bytes 1572872 | tf_op jit(solution)/shard_map/ppermute | solution.py:140
  264.2 21.9 %collective-permute-start.75 = (bf16[2,512,256]{2,1,0:T(8,128)(2,1)}, bf16[2,512,256]{2,1,0:T(8,128)(2,1)}, u32[]{:S(2)}, u32[]{:S(2)}) collective-permute-start(bf16[2,512,256]{2,1,0:T(8,128)(2,1)} %collective-permute-done.74.refs_8_), channel_id=1, source_target_pairs={{0,4},{4,0},{8,12},{12,8},{16,20},{20,16},{24,28},{28,24},{1,5},{5... | collective-permute-start | bytes 1572872 | tf_op jit(solution)/shard_map/ppermute | solution.py:140
  264.3 21.8 %collective-permute-start.73 = (bf16[2,512,256]{2,1,0:T(8,128)(2,1)}, bf16[2,512,256]{2,1,0:T(8,128)(2,1)}, u32[]{:S(2)}, u32[]{:S(2)}) collective-permute-start(bf16[2,512,256]{2,1,0:T(8,128)(2,1)} %collective-permute-done.72.refs_6_), channel_id=1, source_target_pairs={{0,4},{4,0},{8,12},{12,8},{16,20},{20,16},{24,28},{28,24},{1,5},{5... | collective-permute-start | bytes 1572872 | tf_op jit(solution)/shard_map/ppermute | solution.py:140
  (107 other events, 2070.2 us)
